TPU v7x, 32 devices: a 4x4x1 block of a 4x4x8 slice. The times are simulated.
32 devices in a mesh: dp: 2 (over z, core), ep: 16 (over x, y).
Axes of the slice: x: 4, y: 4, z: 1, core: 2. Of those that a mesh axis runs over, the one named last changes fastest.
The devices are a block of a 4x4x8 slice.
Arguments:
- x: bfloat16 [2, 16, 256, 2048], P('dp', 'ep'), parts along dimension 0
- expert: int32 [2, 16, 256, 6], P('dp', 'ep'), parts along dimension 0
- slot: int32 [2, 16, 256, 6], P('dp', 'ep'), parts along dimension 0
- gate: float32 [2, 16, 256, 6], P('dp', 'ep'), parts along dimension 0
- w_gate: bfloat16 [64, 2048, 1408], P('ep')
- w_up: bfloat16 [64, 2048, 1408], P('ep')
- w_down: bfloat16 [64, 1408, 2048], P('ep')
- s_gate: bfloat16 [2048, 2816], replicated
- s_up: bfloat16 [2048, 2816], replicated
- s_down: bfloat16 [2816, 2048], replicated
Outputs:
- y: bfloat16 [2, 16, 256, 2048], P('dp', 'ep'), parts along dimension 0
There are 2 independent parts. A program takes and returns all parts, laid end to end along the dimension named above; an argument that names none is the same for every part.
All inputs are finite; a program needn't handle non-finite values.
Results may differ from a plain program's by a relative error of at most 0.009.
Values are sent between devices in bfloat16 or wider.
A program may use at most 768 MiB of HBM per device.

v0:
```python
import jax
import jax.numpy as jnp
from jax import lax
from jax.sharding import NamedSharding, PartitionSpec as P


def einsum(form, a, b):
    return jnp.einsum(form, a.astype(jnp.float32), b.astype(jnp.float32))


def for_all(x, s_gate, s_up, s_down):
    h = jax.nn.silu(einsum("...d,df->...f", x, s_gate)) * einsum("...d,df->...f", x, s_up)
    return einsum("...f,fd->...d", h.astype(jnp.bfloat16), s_down)


def solution(mesh):
    def placed(v, *spec):
        return lax.with_sharding_constraint(v, NamedSharding(mesh, P(*spec)))

    def step(x, expert, slot, gate, w_gate, w_up, w_down, s_gate, s_up, s_down):
        experts, (tokens, top) = w_gate.shape[0], expert.shape[2:]
        slots = 5 * tokens * top // (4 * experts)
        to_expert = jax.nn.one_hot(expert, experts, dtype=jnp.bfloat16)
        to_slot = jax.nn.one_hot(slot, slots, dtype=jnp.bfloat16)
        weighted = to_expert * gate[..., None].astype(jnp.bfloat16)
        dispatch = einsum("abtke,abtkc->abtec", to_expert, to_slot).astype(jnp.bfloat16)
        combine = einsum("abtke,abtkc->abtec", weighted, to_slot).astype(jnp.bfloat16)
        z = einsum("abtec,abtd->aebcd", dispatch, x).astype(jnp.bfloat16)
        z = placed(z, "dp", None, "ep", None, None)
        z = placed(z, "dp", "ep", None, None, None)
        h = jax.nn.silu(einsum("aebcd,edf->aebcf", z, w_gate))
        h = (h * einsum("aebcd,edf->aebcf", z, w_up)).astype(jnp.bfloat16)
        out = einsum("aebcf,efd->aebcd", h, w_down).astype(jnp.bfloat16)
        out = placed(out, "dp", "ep", None, None, None)
        out = placed(out, "dp", None, "ep", None, None)
        y = einsum("abtec,aebcd->abtd", combine, out)
        return (y + for_all(x, s_gate, s_up, s_down)).astype(jnp.bfloat16)

    return step
```

profile of v0, /device:TPU:112, one launch (start us, length us, event | category | flops | bytes accessed | tf_op | source)
XLA Modules:
  0.0 411.9 jit_solution(15399667908056887646)
XLA Ops:
  0.0 0.0 copy-start
  0.0 0.9 copy.21
  0.9 0.8 copy.23
  1.7 2.6 convolution_convert_fusion.2
  4.4 0.0 copy-done
  4.4 6.2 %convolution_convert_fusion = bf16[64,30,2048]{2,0,1:T(8,128)(2,1)} fusion(bf16[256,64,30]{1,2,0:T(8,128)(2,1)S(1)} %convolution_convert_fusion.2, bf16[1,1,256,2048]{3,2,1,0:T(8,128)(2,1)S(1)} %copy-done), kind=kOutput, calls=%fused_computation.19 | convolution fusion | flops 2017198080 | bytes 9895936 | tf_op jit(solution)/abtec,abtd->aebcd/dot_general | solution.py:8
  10.6 12.4 %reshape.6 = bf16[1,16,4,1,30,2048]{5,2,1,4,3,0:T(4,128)(2,1)} reshape(bf16[64,30,2048]{2,0,1:T(8,128)(2,1)} %convolution_convert_fusion) | data formatting | bytes 15728640 | tf_op jit(solution)/sharding_constraint;jit(solution)/sharding_constraint | solution.py:18
  23.0 12.1 %copy.13 = bf16[1,16,4,1,30,2048]{5,2,4,3,0,1:T(4,128)(2,1)} copy(bf16[1,16,4,1,30,2048]{5,2,1,4,3,0:T(4,128)(2,1)} %reshape.6) | data formatting | bytes 15728640 | tf_op jit(solution)/sharding_constraint;jit(solution)/sharding_constraint | solution.py:18
  35.1 99.9 %all-to-all.4 = bf16[1,16,4,1,30,2048]{5,2,4,3,0,1:T(4,128)(2,1)} all-to-all(bf16[1,16,4,1,30,2048]{5,2,4,3,0,1:T(4,128)(2,1)} %copy.13), channel_id=1, replica_groups=mesh['dp'=2,'ep'=16] {'ep'}, dimensions={1} | all-to-all | bytes 15728640 | tf_op jit(solution)/sharding_constraint;jit(solution)/sharding_constraint | solution.py:18
  135.0 42.4 %fusion.2 = f32[4,16,30,1408]{3,2,1,0:T(8,128)} fusion(bf16[4,2048,1408]{2,1,0:T(8,128)(2,1)} %param.5, bf16[1,16,4,1,30,2048]{5,2,4,3,0,1:T(4,128)(2,1)} %all-to-all.4), kind=kOutput, calls=%fused_computation.2 | convolution fusion | flops 11072962560 | bytes 41746432 | tf_op jit(solution)/aebcd,edf->aebcf/dot_general | solution.py:8
  177.4 44.8 %fusion.6 = bf16[1,4,16,30,1408]{4,3,2,1,0:T(8,128)(2,1)} fusion(f32[4,16,30,1408]{3,2,1,0:T(8,128)} %fusion.2, bf16[4,2048,1408]{2,1,0:T(8,128)(2,1)} %param.4, bf16[1,16,4,1,30,2048]{5,2,4,3,0,1:T(4,128)(2,1)} %all-to-all.4), kind=kOutput, calls=%fused_computation.7 | convolution fusion | flops 11089182720 | bytes 47153152 | tf_op jit(solution)/aebcd,edf->aebcf/dot_general | solution.py:8
  222.1 21.5 %convert_bitcast_fusion = bf16[1,4,16,1,30,2048]{5,4,2,1,3,0:T(8,128)(2,1)} fusion(bf16[4,1408,2048]{2,1,0:T(8,128)(2,1)} %param.6, bf16[1,4,16,30,1408]{4,3,2,1,0:T(8,128)(2,1)} %fusion.6), kind=kOutput, calls=%fused_computation.15 | convolution fusion | flops 11076894720 | bytes 36339712 | tf_op jit(solution)/aebcf,efd->aebcd/dot_general | solution.py:8
  243.6 10.5 %copy.15 = bf16[1,4,16,1,30,2048]{5,1,4,3,0,2:T(4,128)(2,1)} copy(bf16[1,4,16,1,30,2048]{5,4,2,1,3,0:T(8,128)(2,1)} %convert_bitcast_fusion) | data formatting | bytes 15728640 | tf_op jit(solution)/sharding_constraint;jit(solution)/sharding_constraint | solution.py:18
  254.1 0.0 copy-start.1
  254.1 7.6 %all-to-all-start.1 = ((bf16[1,4,16,1,30,2048]{5,1,4,3,0,2:T(4,128)(2,1)}), bf16[1,4,16,1,30,2048]{5,1,4,3,0,2:T(4,128)(2,1)}, u32[]{:S(2)}, u32[]{:S(2)}) async-start(bf16[1,4,16,1,30,2048]{5,1,4,3,0,2:T(4,128)(2,1)} %copy.15), calls=%async_computation.1 | async-start | bytes 15728640 | tf_op jit(solution)/sharding_constraint;jit(solution)/sharding_constraint | solution.py:18
  261.7 0.0 copy-done.1
  261.7 0.1 copy.22
  261.9 3.0 convolution_convert_fusion.1
  264.9 9.0 %convolution_bitcast_fusion.1 = f32[1,1,256,2816]{3,2,1,0:T(8,128)} fusion(bf16[2048,2816]{1,0:T(8,128)(2,1)} %param.7, bf16[1,1,256,2048]{3,2,1,0:T(8,128)(2,1)S(1)} %copy-done), kind=kOutput, calls=%fused_computation.22 | convolution fusion | flops 2952790016 | bytes 15466496 | tf_op jit(solution)/...d,df->...f/dot_general | solution.py:8
  273.8 15.9 %fusion.39 = f32[256,2048]{1,0:T(8,128)} fusion(bf16[2816,2048]{1,0:T(8,128)(2,1)} %param.9, bf16[2048,2816]{1,0:T(8,128)(2,1)} %param.8, f32[1,1,256,2816]{3,2,1,0:T(8,128)} %convolution_bitcast_fusion.1, bf16[1,1,256,2048]{3,2,1,0:T(8,128)(2,1)S(1)} %copy-done), kind=kOutput, calls=%fused_computation.41 | convolution fusion | flops 5909905408 | bytes 29097984 | tf_op jit(solution)/...f,fd->...d/dot_general | solution.py:8
  289.7 90.3 %all-to-all-done.1 = bf16[1,4,16,1,30,2048]{5,1,4,3,0,2:T(4,128)(2,1)} async-done(((bf16[1,4,16,1,30,2048]{5,1,4,3,0,2:T(4,128)(2,1)}), bf16[1,4,16,1,30,2048]{5,1,4,3,0,2:T(4,128)(2,1)}, u32[]{:S(2)}, u32[]{:S(2)}) %all-to-all-start.1) | async-done | bytes 7864352 | tf_op jit(solution)/sharding_constraint;jit(solution)/sharding_constraint | solution.py:18
  380.0 12.1 %copy.16 = bf16[1,16,4,1,30,2048]{5,2,1,4,3,0:T(4,128)(2,1)} copy(bf16[1,16,4,1,30,2048]{5,2,4,3,0,1:T(4,128)(2,1)} %bitcast.21) | data formatting | bytes 15728640 | tf_op jit(solution)/sharding_constraint;jit(solution)/sharding_constraint | solution.py:18
  392.2 11.9 %reshape.46 = bf16[64,30,2048]{2,0,1:T(8,128)(2,1)} reshape(bf16[1,16,4,1,30,2048]{5,2,1,4,3,0:T(4,128)(2,1)} %copy.16) | data formatting | bytes 15728640
  404.0 7.7 %fusion.26 = bf16[1,1,256,2048]{3,2,1,0:T(8,128)(2,1)} fusion(f32[256,2048]{1,0:T(8,128)} %fusion.39, bf16[64,30,2048]{2,0,1:T(8,128)(2,1)} %reshape.46, bf16[256,64,30]{1,2,0:T(8,128)(2,1)S(1)} %convolution_convert_fusion.1), kind=kOutput, calls=%fused_computation.28 | convolution fusion | flops 2014314496 | bytes 11993088 | tf_op jit(solution)/abtec,aebcd->abtd/dot_general | solution.py:8
  (1 shorter events, 0.0 us)
Async XLA Ops:
  0.0 4.4 %copy-start = (bf16[1,1,256,2048]{3,2,1,0:T(8,128)(2,1)S(1)}, bf16[1,1,256,2048]{3,2,1,0:T(8,128)(2,1)}, u32[]{:S(2)}) copy-start(bf16[1,1,256,2048]{3,2,1,0:T(8,128)(2,1)} %param.3) | copy-start | bytes 3145732
  254.1 7.6 %copy-start.1 = (f32[1,1,256,6]{2,1,3,0:T(1,128)S(1)}, f32[1,1,256,6]{2,1,3,0:T(1,128)}, u32[]{:S(2)}) copy-start(f32[1,1,256,6]{2,1,3,0:T(1,128)} %param.1) | copy-start | bytes 18436
  254.1 125.9 %all-to-all-start.1 = ((bf16[1,4,16,1,30,2048]{5,1,4,3,0,2:T(4,128)(2,1)}), bf16[1,4,16,1,30,2048]{5,1,4,3,0,2:T(4,128)(2,1)}, u32[]{:S(2)}, u32[]{:S(2)}) async-start(bf16[1,4,16,1,30,2048]{5,1,4,3,0,2:T(4,128)(2,1)} %copy.15), calls=%async_computation.1 | async-start | bytes 15728640 | tf_op jit(solution)/sharding_constraint;jit(solution)/sharding_constraint | solution.py:18
where the time goes:
time: 419 us; the launch traced here: 412 us
  matrix products  153 us (37%)
  blocking collectives  99.9 us (24%)
  waiting for transfers between devices  90.3 us (22%)
  local copies, waits for them, and re-layouts  61 us (15%)
  starting transfers between devices  7.58 us (2%)
    dot_general x9, matrix products, einsum(): return jnp.einsum(form, a.astype(jnp.float32), b.astype(jnp.float32))  153 us
    another operation x1, blocking collectives, placed(): return lax.with_sharding_constraint(v, NamedSharding(mesh, P(*spec)))  99.9 us
    another operation x1, waiting for transfers between devices, placed(): return lax.with_sharding_constraint(v, NamedSharding(mesh, P(*spec)))  90.3 us
    another operation x4, local copies, waits for them, and re-layouts, placed(): return lax.with_sharding_constraint(v, NamedSharding(mesh, P(*spec)))  47.2 us
    unnamed x7, local copies, waits for them, and re-layouts  13.6 us
  transfers between devices with their start and end apart: 1, of which 1 were waited for; matrix products, arithmetic and copies ran while one was open for 7% of the time, Pallas kernels for 0%

commit v1 on v0

v1 whole, which is shorter than its diff:
```python
import functools
import math

import jax
import jax.numpy as jnp
from jax import lax
from jax.experimental import pallas as pl
from jax.experimental.pallas import tpu as pltpu
from jax.sharding import PartitionSpec as P

MESH = pl.DeviceIdType.MESH
F32, BF16 = jnp.float32, jnp.bfloat16


def dot(a, b):
    return jnp.dot(a, b, preferred_element_type=F32)


def gated(g, u):
    return (jax.nn.silu(g) * u).astype(BF16)


class Place:
    def __init__(self, side):
        me = lax.axis_index("ep")
        self.side = side
        self.x, self.y = lax.div(me, side), lax.rem(me, side)

    def peer(self, axis, d):
        if axis == 0:
            c = lax.rem(self.x + d, self.side)
            return c, {"ep": c * self.side + self.y}
        c = lax.rem(self.y + d, self.side)
        return c, {"ep": self.x * self.side + c}

    def greet(self):
        barrier = pltpu.get_barrier_semaphore()
        for axis in (0, 1):
            for d in range(1, self.side):
                pl.semaphore_signal(barrier, inc=1, device_id=self.peer(axis, d)[1], device_id_type=MESH)
        pl.semaphore_wait(barrier, 2 * (self.side - 1))


def remote(src, dst, sems, k, device):
    return pltpu.make_async_remote_copy(
        src_ref=src, dst_ref=dst, send_sem=sems[0].at[k], recv_sem=sems[1].at[k], device_id=device, device_id_type=MESH
    )


def dispatch_kernel(side, x_ref, ra_ref, rb_ref, sg_ref, su_ref, sd_ref, z_ref, ga_ref, gb_ref, sh_ref,
                    gxa, gxb, sta, stb, s1s, s1r, s2s, s2r, loc):
    at = Place(side)
    tokens, half = gxa.shape[1:]
    local = z_ref.shape[0]
    pad = z_ref.shape[3]
    at.greet()

    first = []
    for axis, (lo, gx, r, g) in enumerate(((0, gxa, ra_ref, ga_ref), (half, gxb, rb_ref, gb_ref))):
        mine = (at.x, at.y)[axis]
        for d in range(1, side):
            c, device = at.peer(axis, d)
            k = (axis * side + d) * 2
            first.append(remote(r.at[c], g.at[mine], (s1s, s1r), k, device))
            first.append(remote(x_ref.at[:, pl.ds(lo, half)], gx.at[mine], (s1s, s1r), k + 1, device))
    for c in first:
        c.start()
    gxa[at.x] = x_ref[:, :half]
    gxb[at.y] = x_ref[:, half:]
    ga_ref[at.x] = ra_ref[at.x]
    gb_ref[at.y] = rb_ref[at.y]

    sh_ref[...] = jnp.zeros_like(sh_ref)

    def shared(g_ref, u_ref, d_ref):
        x = x_ref[...]
        sh_ref[...] += dot(gated(dot(x, g_ref[...]), dot(x, u_ref[...])), d_ref[...])

    d_model, ff = sg_ref.shape
    tile = 256 if ff % 256 == 0 else 128
    pltpu.emit_pipeline(
        shared,
        grid=(ff // tile,),
        in_specs=[
            pl.BlockSpec((d_model, tile), lambda i: (0, i)),
            pl.BlockSpec((d_model, tile), lambda i: (0, i)),
            pl.BlockSpec((tile, d_model), lambda i: (i, 0)),
        ],
    )(sg_ref, su_ref, sd_ref)

    for c in first:
        c.wait()

    def second(e):
        out, own = [], []
        for axis, st in enumerate((sta, stb)):
            for d in range(side):
                c, device = at.peer(1 - axis, d)
                if axis == 0:
                    dst = z_ref.at[e, at.y, :, :, pl.ds(0, half)]
                else:
                    dst = z_ref.at[e, :, at.x, :, pl.ds(half, half)]
                if d == 0:
                    own.append(pltpu.make_async_copy(st.at[e, c], dst, loc.at[e, axis]))
                else:
                    out.append(remote(st.at[e, c], dst, (s2s, s2r), (e * 2 + axis) * side + d, device))
        return out, own

    token = lax.broadcasted_iota(jnp.int32, (tokens, side * pad), 0).astype(F32) + 1.0

    @pl.loop(0, local)
    def _(e):
        for gx, g, st in ((gxa, ga_ref, sta), (gxb, gb_ref, stb)):
            for s in range(side):
                pick = (token == g[s, pl.ds(e, 1), :]).astype(BF16)
                rows = lax.dot_general(pick, gx[s], (((0,), (0,)), ((), ())), preferred_element_type=F32)
                rows = rows.astype(BF16)
                for c in range(side):
                    st[e, c, s] = rows[c * pad : (c + 1) * pad]
        out, own = second(e)
        for c in out + own:
            c.start()

    @pl.loop(0, local)
    def _(e):
        out, own = second(e)
        for c in out + own:
            c.wait()


def expert_kernel(z_ref, wg_ref, wu_ref, wd_ref, out_ref, h_ref):
    z = z_ref[0]
    ff, d_model = wd_ref.shape[1:]
    for lo in range(0, ff, 512):
        hi = min(lo + 512, ff)
        h_ref[:, lo:hi] = gated(dot(z, wg_ref[0, :, lo:hi]), dot(z, wu_ref[0, :, lo:hi]))
    for lo in range(0, d_model, 512):
        hi = min(lo + 512, d_model)
        out_ref[0, :, lo:hi] = dot(h_ref[...], wd_ref[0, :, lo:hi]).astype(BF16)


def combine_kernel(side, o_ref, ga_ref, gb_ref, sh_ref, y_ref, ca, cb, pa, pb, qa, qb, ta, tb, s1s, s1r, s2s, s2r, loc):
    at = Place(side)
    local = ca.shape[0]
    pad, half = ca.shape[3:]
    tokens = pa.shape[1]
    at.greet()

    def first(e):
        out, own = [], []
        for axis in (0, 1):
            for d in range(side):
                c, device = at.peer(1 - axis, d)
                if axis == 0:
                    src, dst = o_ref.at[e, c, :, :, pl.ds(0, half)], ca.at[e, :, at.y]
                else:
                    src, dst = o_ref.at[e, :, c, :, pl.ds(half, half)], cb.at[e, :, at.x]
                if d == 0:
                    own.append(pltpu.make_async_copy(src, dst, loc.at[e, axis]))
                else:
                    out.append(remote(src, dst, (s1s, s1r), (e * 2 + axis) * side + d, device))
        return out + own

    @pl.loop(0, local)
    def _(e):
        for c in first(e):
            c.start()

    pa[...] = jnp.zeros_like(pa)
    pb[...] = jnp.zeros_like(pb)
    token = lax.broadcasted_iota(jnp.int32, (tokens, side * pad), 0).astype(F32) + 1.0

    @pl.loop(0, local)
    def _(e):
        for c in first(e):
            c.wait()
        for p, g, rows in ((pa, ga_ref, ca), (pb, gb_ref, cb)):
            for s in range(side):
                weigh = jnp.where(token == g[s, pl.ds(e, 1), :], g[s, pl.ds(local + e, 1), :], 0.0).astype(BF16)
                p[s] += dot(weigh, rows[e, s].reshape(side * pad, half))

    second = []
    for axis, (p, t, q) in enumerate(((pa, ta, qa), (pb, tb, qb))):
        t[...] = p[...].astype(BF16)
        mine = (at.x, at.y)[axis]
        for d in range(1, side):
            c, device = at.peer(axis, d)
            second.append(remote(t.at[c], q.at[mine], (s2s, s2r), axis * side + d, device))
    for c in second:
        c.start()
    for c in second:
        c.wait()
    for axis, (p, q, lo) in enumerate(((pa, qa, 0), (pb, qb, half))):
        mine = (at.x, at.y)[axis]
        y = p[mine]
        for d in range(1, side):
            y += q[at.peer(axis, d)[0]].astype(F32)
        y_ref[:, lo : lo + half] = (y + sh_ref[:, lo : lo + half]).astype(BF16)


def solution(mesh):
    side = math.isqrt(mesh.shape["ep"])
    vmem, hbm = pl.BlockSpec(memory_space=pltpu.VMEM), pl.BlockSpec(memory_space=pl.ANY)
    dma = lambda *n: pltpu.SemaphoreType.DMA(n)
    limit = 62 << 20

    def body(x, expert, slot, gate, w_gate, w_up, w_down, s_gate, s_up, s_down):
        x, expert, slot, gate = x[0, 0], expert[0, 0], slot[0, 0], gate[0, 0]
        tokens, top = expert.shape
        d_model = x.shape[1]
        local, _, ff = w_gate.shape
        experts = local * side * side
        slots = 5 * tokens * top // (4 * experts)
        pad = -(-slots // 16) * 16
        half = d_model // 2
        assert tokens <= 256

        to_expert = jax.nn.one_hot(expert.reshape(-1), experts, dtype=BF16)
        slot = slot.reshape(-1)
        to_slot = jax.nn.one_hot(jnp.where(slot < slots, slot, pad), pad, dtype=BF16)
        number = jnp.repeat(jnp.arange(1, tokens + 1), top).astype(BF16)[:, None]
        held = jnp.concatenate([to_slot * number, to_slot * gate.reshape(-1).astype(BF16)[:, None]], axis=1)
        held = lax.dot_general(to_expert, held, (((0,), (0,)), ((), ())), preferred_element_type=F32)
        held = held.reshape(side, side, local, 2, pad)
        ra = held.transpose(0, 3, 2, 1, 4).reshape(side, 2 * local, side * pad)
        rb = held.transpose(1, 3, 2, 0, 4).reshape(side, 2 * local, side * pad)

        shape = jax.ShapeDtypeStruct
        z, ga, gb, sh = pl.pallas_call(
            functools.partial(dispatch_kernel, side),
            out_shape=(
                shape((local, side, side, pad, d_model), BF16),
                shape(ra.shape, F32),
                shape(rb.shape, F32),
                shape((tokens, d_model), F32),
            ),
            in_specs=[vmem, vmem, vmem, hbm, hbm, hbm],
            out_specs=(hbm, vmem, vmem, vmem),
            scratch_shapes=[
                pltpu.VMEM((side, tokens, half), BF16),
                pltpu.VMEM((side, tokens, half), BF16),
                pltpu.VMEM((local, side, side, pad, half), BF16),
                pltpu.VMEM((local, side, side, pad, half), BF16),
                dma(4 * side),
                dma(4 * side),
                dma(2 * local * side),
                dma(2 * local * side),
                dma(local, 2),
            ],
            compiler_params=pltpu.CompilerParams(collective_id=0, has_side_effects=True, vmem_limit_bytes=limit),
        )(x, ra, rb, s_gate, s_up, s_down)

        rows = side * side * pad
        out = pl.pallas_call(
            expert_kernel,
            grid=(local,),
            out_shape=shape((local, rows, d_model), BF16),
            in_specs=[
                pl.BlockSpec((1, rows, d_model), lambda e: (e, 0, 0)),
                pl.BlockSpec((1, d_model, ff), lambda e: (e, 0, 0)),
                pl.BlockSpec((1, d_model, ff), lambda e: (e, 0, 0)),
                pl.BlockSpec((1, ff, d_model), lambda e: (e, 0, 0)),
            ],
            out_specs=pl.BlockSpec((1, rows, d_model), lambda e: (e, 0, 0)),
            scratch_shapes=[pltpu.VMEM((rows, ff), BF16)],
            compiler_params=pltpu.CompilerParams(vmem_limit_bytes=limit),
        )(z.reshape(local, rows, d_model), w_gate, w_up, w_down)

        y = pl.pallas_call(
            functools.partial(combine_kernel, side),
            out_shape=shape((tokens, d_model), BF16),
            in_specs=[hbm, vmem, vmem, vmem],
            out_specs=vmem,
            scratch_shapes=[
                pltpu.VMEM((local, side, side, pad, half), BF16),
                pltpu.VMEM((local, side, side, pad, half), BF16),
                pltpu.VMEM((side, tokens, half), F32),
                pltpu.VMEM((side, tokens, half), F32),
                pltpu.VMEM((side, tokens, half), BF16),
                pltpu.VMEM((side, tokens, half), BF16),
                pltpu.VMEM((side, tokens, half), BF16),
                pltpu.VMEM((side, tokens, half), BF16),
                dma(2 * local * side),
                dma(2 * local * side),
                dma(2 * side),
                dma(2 * side),
                dma(local, 2),
            ],
            compiler_params=pltpu.CompilerParams(collective_id=1, has_side_effects=True, vmem_limit_bytes=limit),
        )(out.reshape(z.shape), ga, gb, sh)
        return y[None, None]

    token = P("dp", "ep")
    return jax.shard_map(
        body,
        mesh=mesh,
        in_specs=(token,) * 4 + (P("ep"),) * 3 + (P(),) * 3,
        out_specs=token,
        check_vma=False,
    )
```

time: 419 us -> 217 us (0.52)
  the two profiles are of different devices: /device:TPU:112 before, /device:TPU:96 now
where the time goes in v1:
time: 217 us
  Pallas kernels  208 us (96%)
  local copies, waits for them, and re-layouts  6.33 us (3%)
    pallas_call x1, Pallas kernels, body(): pl.pallas_call(functools.partial(dispatch_kernel, side), out_shape=(shape...  81.4 us
    pallas_call x1, Pallas kernels, body(): pl.pallas_call(functools.partial(combine_kernel, side), out_shape=shape((...  78.6 us
    pallas_call x1, Pallas kernels, body(): pl.pallas_call(expert_kernel, grid=(local,), out_shape=shape((local, rows...  47.6 us

profile of v1, /device:TPU:96, one launch (start us, length us, event | category | flops | bytes accessed | tf_op | source)
XLA Modules:
  0.0 216.7 jit_solution(15840139603118339154)
XLA Ops:
  0.0 0.7 convert_element_type.27
  0.7 0.1 copy.15
  0.9 0.2 convert_element_type.28
  1.0 0.1 broadcast_in_dim.17
  1.1 0.2 convert_element_type.26
  1.3 0.8 copy.13
  2.1 0.1 eq.42
  2.2 0.8 copy.14
  3.1 0.1 reshape_squeeze.2
  3.2 1.2 fusion.1
  4.4 0.7 fusion.2
  5.1 0.1 reshape.39
  5.3 0.7 reshape.40.ra_ref
  6.0 0.7 reshape.41.rb_ref
  6.7 81.4 %shard_map.100 = (bf16[4,4,4,32,2048]{4,3,2,1,0:T(8,128)(2,1)}, f32[4,8,128]{2,1,0:T(8,128)}, f32[4,8,128]{2,1,0:T(8,128)}, f32[256,2048]{1,0:T(8,128)}) custom-call(bf16[256,2048]{1,0:T(8,128)(2,1)} %bitcast.19, f32[4,8,128]{2,1,0:T(8,128)} %reshape.40.ra_ref, f32[4,8,128]{2,1,0:T(8,128)} %reshape.41.rb_ref, bf16[2048,2816]{1,0:T(8,128)(2,1)} %sg_ref.1, ...), custom_call_target="tpu_custom_call" | custom-call | tf_op jit(solution)/shard_map/pallas_call | solution.py:229
  88.1 47.6 %shard_map.101 = bf16[4,512,2048]{2,1,0:T(8,128)(2,1)} custom-call(bf16[4,512,2048]{2,1,0:T(8,128)(2,1)} %bitcast.17, bf16[4,2048,1408]{2,1,0:T(8,128)(2,1)} %wg_ref.1, bf16[4,2048,1408]{2,1,0:T(8,128)(2,1)} %wu_ref.1, bf16[4,1408,2048]{2,1,0:T(8,128)(2,1)} %wd_ref.1), custom_call_target="tpu_custom_call" | custom-call | tf_op jit(solution)/shard_map/pallas_call | solution.py:254
  135.7 78.6 %shard_map.102 = bf16[256,2048]{1,0:T(8,128)(2,1)} custom-call(bf16[4,4,4,32,2048]{4,3,2,1,0:T(8,128)(2,1)} %bitcast.16, f32[4,8,128]{2,1,0:T(8,128)} %get-tuple-element.10.ga_ref, f32[4,8,128]{2,1,0:T(8,128)} %get-tuple-element.11.gb_ref, f32[256,2048]{1,0:T(8,128)} %get-tuple-element.12.sh_ref), custom_call_target="tpu_custom_call" | custom-call | tf_op jit(solution)/shard_map/pallas_call | solution.py:269
  214.4 2.3 %copy.23 = bf16[1,1,256,2048]{3,2,1,0:T(8,128)(2,1)} copy(bf16[1,1,256,2048]{3,2,1,0:T(8,128)(2,1)} %bitcast.18) | data formatting | bytes 2097152
  (4 shorter events, 0.1 us)

commit v2 on v1

v2 whole, which is shorter than its diff:
```python
import functools
import math

import jax
import jax.numpy as jnp
from jax import lax
from jax.experimental import pallas as pl
from jax.experimental.pallas import tpu as pltpu
from jax.sharding import PartitionSpec as P

MESH = pl.DeviceIdType.MESH
F32, BF16 = jnp.float32, jnp.bfloat16
UP, DOWN = 128, 512
DEPTH = 3


def dot(a, b, contract=((1,), (0,))):
    return lax.dot_general(a, b, (contract, ((), ())), preferred_element_type=F32)


def gated(g, u):
    return (jax.nn.silu(g) * u).astype(BF16)


class Place:
    def __init__(self, side):
        me = lax.axis_index("ep")
        self.side = side
        self.x, self.y = lax.div(me, side), lax.rem(me, side)

    def peer(self, axis, d):
        if axis == 0:
            c = lax.rem(self.x + d, self.side)
            return c, {"ep": c * self.side + self.y}
        c = lax.rem(self.y + d, self.side)
        return c, {"ep": self.x * self.side + c}

    def greet(self):
        barrier = pltpu.get_barrier_semaphore()
        for axis in (0, 1):
            for d in range(1, self.side):
                pl.semaphore_signal(barrier, inc=1, device_id=self.peer(axis, d)[1], device_id_type=MESH)
        pl.semaphore_wait(barrier, 2 * (self.side - 1))


def remote(src, dst, sems, k, device):
    return pltpu.make_async_remote_copy(
        src_ref=src, dst_ref=dst, send_sem=sems[0].at[k], recv_sem=sems[1].at[k], device_id=device, device_id_type=MESH
    )


def tables(side, local, pad, slots, expert, slot, gate, ra, rb):
    top, tokens = expert.shape
    token = lax.broadcasted_iota(jnp.int32, (1, tokens), 1).astype(F32) + 1.0
    lines = lax.broadcasted_iota(jnp.int32, (side * local, tokens), 0)
    places = lax.broadcasted_iota(jnp.int32, (side * pad, tokens), 0)
    sums = [0.0, 0.0]
    for k in range(top):
        ex, sl = expert[k : k + 1], slot[k : k + 1]
        weight = gate[k : k + 1].astype(BF16).astype(F32)
        e, device = lax.rem(ex, local), lax.div(ex, local)
        where = lax.div(device, side), lax.rem(device, side)
        for axis in (0, 1):
            line = (lines == where[axis] * local + e).astype(F32).astype(BF16)
            hit = places == jnp.where(sl < slots, where[1 - axis] * pad + sl, -1)
            held = jnp.concatenate([jnp.where(hit, token, 0.0), jnp.where(hit, weight, 0.0)]).astype(BF16)
            sums[axis] += dot(line, held, ((1,), (1,)))
    for held, r in zip(sums, (ra, rb)):
        for c in range(side):
            r[c, :local] = held[c * local : (c + 1) * local, : side * pad]
            r[c, local:] = held[c * local : (c + 1) * local, side * pad :]


def layer_kernel(side, slots, x_ref, ex_ref, sl_ref, gt_ref, sg_ref, su_ref, sd_ref, wg_ref, wu_ref, wd_ref, y_ref,
                 ra, rb, ga, gb, gxa, gxb, sta, stb, z, h, ca, cb, pa, pb, ta, tb, qa, qb, sh, wup, wdn,
                 s1s, s1r, s2s, s2r, s3s, s3r, s4s, s4r, loc2, loc3, sup, sdn):
    at = Place(side)
    tokens, half = gxa.shape[1:]
    local, pad = z.shape[0], z.shape[3]
    rows = side * side * pad
    d_model, ff = wg_ref.shape[1:]
    ups, downs = ff // UP, d_model // DOWN

    def up_tile(n):
        e, i = lax.div(n, ups), lax.rem(n, ups)
        k = lax.rem(n, DEPTH)
        cols = pl.ds(pl.multiple_of(i * UP, UP), UP)
        return [
            pltpu.make_async_copy(w.at[e, :, cols], wup.at[k, :, pl.ds(j * UP, UP)], sup.at[k, j])
            for j, w in enumerate((wg_ref, wu_ref))
        ]

    def down_tile(n):
        e, i = lax.div(n, downs), lax.rem(n, downs)
        k = lax.rem(n, 2)
        cols = pl.ds(pl.multiple_of(i * DOWN, DOWN), DOWN)
        return pltpu.make_async_copy(wd_ref.at[e, :, cols], wdn.at[k], sdn.at[k])

    at.greet()

    first, small = [], []
    for axis, (lo, gx, r, g) in enumerate(((0, gxa, ra, ga), (half, gxb, rb, gb))):
        mine = (at.x, at.y)[axis]
        for d in range(1, side):
            c, device = at.peer(axis, d)
            k = (axis * side + d) * 2
            small.append(remote(r.at[c], g.at[mine], (s1s, s1r), k, device))
            first.append(remote(x_ref.at[:, pl.ds(lo, half)], gx.at[mine], (s1s, s1r), k + 1, device))
    for c in first:
        c.start()
    tables(side, local, pad, slots, ex_ref, sl_ref, gt_ref, ra, rb)
    gxa[at.x] = x_ref[:, :half]
    gxb[at.y] = x_ref[:, half:]
    sh[...] = jnp.zeros_like(sh)
    for c in small:
        c.start()
    ga[at.x] = ra[at.x]
    gb[at.y] = rb[at.y]

    def shared(g_ref, u_ref, d_ref):
        x = x_ref[...]
        sh[...] += dot(gated(dot(x, g_ref[...]), dot(x, u_ref[...])), d_ref[...])

    tile = 256 if sg_ref.shape[1] % 256 == 0 else 128
    pltpu.emit_pipeline(
        shared,
        grid=(sg_ref.shape[1] // tile,),
        in_specs=[
            pl.BlockSpec((d_model, tile), lambda i: (0, i)),
            pl.BlockSpec((d_model, tile), lambda i: (0, i)),
            pl.BlockSpec((tile, d_model), lambda i: (i, 0)),
        ],
    )(sg_ref, su_ref, sd_ref)

    for n in range(DEPTH - 1):
        for c in up_tile(jnp.int32(n)):
            c.start()
    down_tile(jnp.int32(0)).start()
    for c in small + first:
        c.wait()

    def second(e):
        out, own = [], []
        for axis, st in enumerate((sta, stb)):
            for d in range(side):
                c, device = at.peer(1 - axis, d)
                if axis == 0:
                    dst = z.at[e, at.y, :, :, pl.ds(0, half)]
                else:
                    dst = z.at[e, :, at.x, :, pl.ds(half, half)]
                if d == 0:
                    own.append(pltpu.make_async_copy(st.at[e, c], dst, loc2.at[e, axis]))
                else:
                    out.append(remote(st.at[e, c], dst, (s2s, s2r), (e * 2 + axis) * side + d, device))
        return out + own

    token = lax.broadcasted_iota(jnp.int32, (tokens, side * pad), 0).astype(F32) + 1.0

    @pl.loop(0, local)
    def _(e):
        for gx, g, st in ((gxa, ga, sta), (gxb, gb, stb)):
            for s in range(side):
                pick = (token == g[s, pl.ds(e, 1), :]).astype(F32).astype(BF16)
                picked = dot(pick, gx[s], ((0,), (0,))).astype(BF16)
                for c in range(side):
                    st[e, c, s] = picked[c * pad : (c + 1) * pad]
        for c in second(e):
            c.start()

    def third(e):
        out, own = [], []
        for axis in (0, 1):
            for d in range(side):
                c, device = at.peer(1 - axis, d)
                if axis == 0:
                    src, dst = z.at[e, c, :, :, pl.ds(0, half)], ca.at[e, :, at.y]
                else:
                    src, dst = z.at[e, :, c, :, pl.ds(half, half)], cb.at[e, :, at.x]
                if d == 0:
                    own.append(pltpu.make_async_copy(src, dst, loc3.at[e, axis]))
                else:
                    out.append(remote(src, dst, (s3s, s3r), (e * 2 + axis) * side + d, device))
        return out + own

    @pl.loop(0, local)
    def _(e):
        for c in second(e):
            c.wait()

        @pl.loop(0, ups)
        def _(i):
            n = e * ups + i

            @pl.when(n + DEPTH - 1 < local * ups)
            def _():
                for c in up_tile(n + DEPTH - 1):
                    c.start()

            for c in up_tile(n):
                c.wait()
            gu = dot(z[e].reshape(rows, d_model), wup[lax.rem(n, DEPTH)])
            h[:, pl.ds(pl.multiple_of(i * UP, UP), UP)] = gated(gu[:, :UP], gu[:, UP:])

        @pl.loop(0, downs)
        def _(i):
            n = e * downs + i

            @pl.when(n + 1 < local * downs)
            def _():
                down_tile(n + 1).start()

            down_tile(n).wait()
            out = dot(h[...], wdn[lax.rem(n, 2)]).astype(BF16)
            z[e, :, :, :, pl.ds(pl.multiple_of(i * DOWN, DOWN), DOWN)] = out.reshape(side, side, pad, DOWN)

        for c in third(e):
            c.start()

    pa[...] = jnp.zeros_like(pa)
    pb[...] = jnp.zeros_like(pb)

    @pl.loop(0, local)
    def _(e):
        for c in third(e):
            c.wait()
        for p, g, back in ((pa, ga, ca), (pb, gb, cb)):
            for s in range(side):
                weigh = jnp.where(token == g[s, pl.ds(e, 1), :], g[s, pl.ds(local + e, 1), :], 0.0).astype(BF16)
                p[s] += dot(weigh, back[e, s].reshape(side * pad, half))

    last = []
    for axis, (p, t, q) in enumerate(((pa, ta, qa), (pb, tb, qb))):
        t[...] = p[...].astype(BF16)
        mine = (at.x, at.y)[axis]
        for d in range(1, side):
            c, device = at.peer(axis, d)
            last.append(remote(t.at[c], q.at[mine], (s4s, s4r), axis * side + d, device))
    for c in last:
        c.start()
    for c in last:
        c.wait()
    for axis, (p, q, lo) in enumerate(((pa, qa, 0), (pb, qb, half))):
        mine = (at.x, at.y)[axis]
        y = p[mine]
        for d in range(1, side):
            y += q[at.peer(axis, d)[0]].astype(F32)
        y_ref[:, lo : lo + half] = (y + sh[:, lo : lo + half]).astype(BF16)


def solution(mesh):
    side = math.isqrt(mesh.shape["ep"])
    vmem, hbm = pl.BlockSpec(memory_space=pltpu.VMEM), pl.BlockSpec(memory_space=pl.ANY)
    dma = lambda *n: pltpu.SemaphoreType.DMA(n)

    def body(x, expert, slot, gate, w_gate, w_up, w_down, s_gate, s_up, s_down):
        x, expert, slot, gate = x[0, 0], expert[0, 0], slot[0, 0], gate[0, 0]
        tokens, top = expert.shape
        d_model = x.shape[1]
        local, _, ff = w_gate.shape
        slots = 5 * tokens * top // (4 * local * side * side)
        pad = -(-slots // 16) * 16
        half = d_model // 2
        assert tokens <= 256
        staged = pltpu.VMEM((local, side, side, pad, half), BF16)
        gathered = pltpu.VMEM((side, tokens, half), BF16)
        added = pltpu.VMEM((side, tokens, half), F32)
        table = pltpu.VMEM((side, 2 * local, side * pad), F32)
        y = pl.pallas_call(
            functools.partial(layer_kernel, side, slots),
            out_shape=jax.ShapeDtypeStruct((tokens, d_model), BF16),
            in_specs=[vmem] * 4 + [hbm] * 6,
            out_specs=vmem,
            scratch_shapes=[table] * 4
            + [gathered] * 2
            + [staged] * 2
            + [pltpu.VMEM((local, side, side, pad, d_model), BF16), pltpu.VMEM((side * side * pad, ff), BF16)]
            + [staged] * 2
            + [added] * 2
            + [gathered] * 4
            + [
                pltpu.VMEM((tokens, d_model), F32),
                pltpu.VMEM((DEPTH, d_model, 2 * UP), BF16),
                pltpu.VMEM((2, ff, DOWN), BF16),
            ]
            + [dma(4 * side)] * 2
            + [dma(2 * local * side)] * 4
            + [dma(2 * side)] * 2
            + [dma(local, 2)] * 2
            + [dma(DEPTH, 2), dma(2)],
            compiler_params=pltpu.CompilerParams(collective_id=0, has_side_effects=True, vmem_limit_bytes=67043328),
        )(x, expert.T, slot.T, gate.T, s_gate, s_up, s_down, w_gate, w_up, w_down)
        return y[None, None]

    token = P("dp", "ep")
    return jax.shard_map(
        body,
        mesh=mesh,
        in_specs=(token,) * 4 + (P("ep"),) * 3 + (P(),) * 3,
        out_specs=token,
        check_vma=False,
    )
```

time: 217 us -> 159 us (0.73)
  Pallas kernels: 208 us -> 154 us
    pallas_call x3 -> x1, Pallas kernels: 208 us -> 154 us  [body(): pl.pallas_call(functools.partial(layer_kernel, side, slots), out_shape=ja...]
where the time goes in v2:
time: 159 us
  Pallas kernels  154 us (97%)
  local copies, waits for them, and re-layouts  4.9 us (3%)
    pallas_call x1, Pallas kernels, body(): pl.pallas_call(functools.partial(layer_kernel, side, slots), out_shape=ja...  154 us
    unnamed x2, local copies, waits for them, and re-layouts  3.59 us

profile of v2, /device:TPU:96, one launch (start us, length us, event | category | flops | bytes accessed | tf_op | source)
XLA Modules:
  0.0 158.6 jit_solution(3950455889477296432)
XLA Ops:
  0.0 1.3 copy.17
  1.3 1.3 copy_bitcast_fusion.1
  2.6 153.7 %shard_map.100 = bf16[256,2048]{1,0:T(8,128)(2,1)} custom-call(bf16[256,2048]{1,0:T(8,128)(2,1)} %bitcast.16, s32[6,256]{1,0:T(8,128)} %get-tuple-element.6.ex_ref, s32[6,256]{1,0:T(8,128)} %get-tuple-element.5.sl_ref, f32[6,256]{1,0:T(8,128)} %bitcast.17, bf16[2048,2816]{1,0:T(8,128)(2,1)} %sg_ref.1, bf16[2048,2816]{1,0:T(8,128)(2,1)} %su_ref.1, ...), custom_call_target="tpu_custom_call" | custom-call | tf_op jit(solution)/shard_map/pallas_call | solution.py:268
  156.3 2.3 %copy.19 = bf16[1,1,256,2048]{3,2,1,0:T(8,128)(2,1)} copy(bf16[1,1,256,2048]{3,2,1,0:T(8,128)(2,1)} %bitcast.15) | data formatting | bytes 2097152

commit v3 on v2

--- a/solution.py
+++ b/solution.py
@@ -10,7 +10,7 @@
 
 MESH = pl.DeviceIdType.MESH
 F32, BF16 = jnp.float32, jnp.bfloat16
-UP, DOWN = 128, 512
+UP, DOWN = 128, 1024
 DEPTH = 3
 
 
@@ -50,14 +50,14 @@
 
 
 def tables(side, local, pad, slots, expert, slot, gate, ra, rb):
-    top, tokens = expert.shape
+    top, _, tokens = expert.shape
     token = lax.broadcasted_iota(jnp.int32, (1, tokens), 1).astype(F32) + 1.0
     lines = lax.broadcasted_iota(jnp.int32, (side * local, tokens), 0)
     places = lax.broadcasted_iota(jnp.int32, (side * pad, tokens), 0)
     sums = [0.0, 0.0]
     for k in range(top):
-        ex, sl = expert[k : k + 1], slot[k : k + 1]
-        weight = gate[k : k + 1].astype(BF16).astype(F32)
+        ex, sl = expert[k], slot[k]
+        weight = gate[k].astype(BF16).astype(F32)
         e, device = lax.rem(ex, local), lax.div(ex, local)
         where = lax.div(device, side), lax.rem(device, side)
         for axis in (0, 1):
@@ -72,8 +72,8 @@
 
 
 def layer_kernel(side, slots, x_ref, ex_ref, sl_ref, gt_ref, sg_ref, su_ref, sd_ref, wg_ref, wu_ref, wd_ref, y_ref,
-                 ra, rb, ga, gb, gxa, gxb, sta, stb, z, h, ca, cb, pa, pb, ta, tb, qa, qb, sh, wup, wdn,
-                 s1s, s1r, s2s, s2r, s3s, s3r, s4s, s4r, loc2, loc3, sup, sdn):
+                 ra, rb, ga, gb, gxa, gxb, sta, stb, z, h, ca, cb, pa, pb, ta, tb, qa, qb, va, vb, sh, wup, wdn,
+                 s0s, s0r, s1s, s1r, s2s, s2r, s3s, s3r, s4s, s4r, loc2, loc3, sup, sdn):
     at = Place(side)
     tokens, half = gxa.shape[1:]
     local, pad = z.shape[0], z.shape[3]
@@ -98,24 +98,73 @@
 
     at.greet()
 
-    first, small = [], []
-    for axis, (lo, gx, r, g) in enumerate(((0, gxa, ra, ga), (half, gxb, rb, gb))):
-        mine = (at.x, at.y)[axis]
+    right, left = 1, side - 1
+    cut = tokens // 2
+    low, high = pl.ds(0, cut), pl.ds(cut, cut)
+    sides = ((0, gxa, ra, ga, at.x), (half, gxb, rb, gb, at.y))
+    first, onward, small = [], [], []
+    for axis, (lo, gx, r, g, mine) in enumerate(sides):
+        cols = pl.ds(lo, half)
+        for i, (d, piece) in enumerate(((right, low), (left, high), (right, high), (left, low))):
+            device = at.peer(axis, d)[1]
+            first.append(remote(x_ref.at[piece, cols], gx.at[mine, piece], (s1s, s1r), axis * 6 + i, device))
+        for i, (d, piece) in enumerate(((right, low), (left, high))):
+            origin = at.peer(axis, side - d)[0]
+            rows_on = gx.at[origin, piece]
+            onward.append(remote(rows_on, rows_on, (s1s, s1r), axis * 6 + 4 + i, at.peer(axis, d)[1]))
         for d in range(1, side):
             c, device = at.peer(axis, d)
-            k = (axis * side + d) * 2
-            small.append(remote(r.at[c], g.at[mine], (s1s, s1r), k, device))
-            first.append(remote(x_ref.at[:, pl.ds(lo, half)], gx.at[mine], (s1s, s1r), k + 1, device))
-    for c in first:
-        c.start()
+            small.append(remote(r.at[c], g.at[mine], (s0s, s0r), axis * side + d, device))
+    for i in (0, 1, 4, 5, 2, 3, 6, 7):
+        first[i].start()
     tables(side, local, pad, slots, ex_ref, sl_ref, gt_ref, ra, rb)
-    gxa[at.x] = x_ref[:, :half]
-    gxb[at.y] = x_ref[:, half:]
-    sh[...] = jnp.zeros_like(sh)
     for c in small:
         c.start()
     ga[at.x] = ra[at.x]
     gb[at.y] = rb[at.y]
+
+    token = lax.broadcasted_iota(jnp.int32, (tokens, side * pad), 0).astype(F32) + 1.0
+
+    def pick(e, axis, c, x):
+        g, st = ((ga, sta), (gb, stb))[axis]
+        hit = (token == g[c, pl.ds(e, 1), :]).astype(F32).astype(BF16)
+        picked = dot(hit, x, ((0,), (0,))).astype(BF16)
+        for to in range(side):
+            st[e, to, c] = picked[to * pad : (to + 1) * pad]
+
+    def second(e, origin=None):
+        out = []
+        for axis, st in enumerate((sta, stb)):
+            piece = slice(None) if origin is None else at.peer(axis, origin)[0]
+            for d in range(side):
+                c, device = at.peer(1 - axis, d)
+                src = st.at[e, c, piece]
+                if axis == 0:
+                    dst = z.at[e, at.y, piece, :, pl.ds(0, half)]
+                else:
+                    dst = z.at[e, piece, at.x, :, pl.ds(half, half)]
+                if d == 0:
+                    out.append(pltpu.make_async_copy(src, dst, loc2.at[e, axis]))
+                else:
+                    out.append(remote(src, dst, (s2s, s2r), (e * 2 + axis) * side + d, device))
+        return out
+
+    @pl.loop(0, local)
+    def _(e):
+        pick(e, 0, at.x, x_ref[:, :half])
+        pick(e, 1, at.y, x_ref[:, half:])
+
+    for i in (0, 1, 4, 5):
+        first[i].wait_recv()
+    for c in onward:
+        c.start()
+
+    @pl.loop(0, local)
+    def _(e):
+        for c in second(e, 0):
+            c.start()
+
+    sh[...] = jnp.zeros_like(sh)
 
     def shared(g_ref, u_ref, d_ref):
         x = x_ref[...]
@@ -136,54 +185,44 @@
         for c in up_tile(jnp.int32(n)):
             c.start()
     down_tile(jnp.int32(0)).start()
-    for c in small + first:
-        c.wait()
-
-    def second(e):
-        out, own = [], []
-        for axis, st in enumerate((sta, stb)):
+    for i in (2, 3, 6, 7):
+        first[i].wait_recv()
+    for c in onward + small:
+        c.wait_recv()
+
+    @pl.loop(0, local)
+    def _(e):
+        for d in range(1, side):
+            for axis, gx in enumerate((gxa, gxb)):
+                c = at.peer(axis, d)[0]
+                pick(e, axis, c, gx[c])
+            for c in second(e, d):
+                c.start()
+
+    for c in first + onward + small:
+        c.wait_send()
+
+    final = local - 1
+
+    def third(e, origin=None):
+        out = []
+        for axis in (0, 1):
+            piece = slice(None) if origin is None else at.peer(axis, origin)[0]
             for d in range(side):
                 c, device = at.peer(1 - axis, d)
                 if axis == 0:
-                    dst = z.at[e, at.y, :, :, pl.ds(0, half)]
+                    src, dst = z.at[e, c, piece, :, pl.ds(0, half)], ca.at[e, piece, at.y]
                 else:
-                    dst = z.at[e, :, at.x, :, pl.ds(half, half)]
+                    src, dst = z.at[e, piece, c, :, pl.ds(half, half)], cb.at[e, piece, at.x]
+                k = (e * 2 + axis) * side + d if origin is None else ((local + origin) * 2 + axis) * side + d
                 if d == 0:
-                    own.append(pltpu.make_async_copy(st.at[e, c], dst, loc2.at[e, axis]))
+                    own = loc3.at[e if origin is None else local + origin, axis]
+                    out.append(pltpu.make_async_copy(src, dst, own))
                 else:
-                    out.append(remote(st.at[e, c], dst, (s2s, s2r), (e * 2 + axis) * side + d, device))
-        return out + own
-
-    token = lax.broadcasted_iota(jnp.int32, (tokens, side * pad), 0).astype(F32) + 1.0
-
-    @pl.loop(0, local)
-    def _(e):
-        for gx, g, st in ((gxa, ga, sta), (gxb, gb, stb)):
-            for s in range(side):
-                pick = (token == g[s, pl.ds(e, 1), :]).astype(F32).astype(BF16)
-                picked = dot(pick, gx[s], ((0,), (0,))).astype(BF16)
-                for c in range(side):
-                    st[e, c, s] = picked[c * pad : (c + 1) * pad]
-        for c in second(e):
-            c.start()
-
-    def third(e):
-        out, own = [], []
-        for axis in (0, 1):
-            for d in range(side):
-                c, device = at.peer(1 - axis, d)
-                if axis == 0:
-                    src, dst = z.at[e, c, :, :, pl.ds(0, half)], ca.at[e, :, at.y]
-                else:
-                    src, dst = z.at[e, :, c, :, pl.ds(half, half)], cb.at[e, :, at.x]
-                if d == 0:
-                    own.append(pltpu.make_async_copy(src, dst, loc3.at[e, axis]))
-                else:
-                    out.append(remote(src, dst, (s3s, s3r), (e * 2 + axis) * side + d, device))
-        return out + own
-
-    @pl.loop(0, local)
-    def _(e):
+                    out.append(remote(src, dst, (s3s, s3r), k, device))
+        return out
+
+    def expert(e):
         for c in second(e):
             c.wait()
 
@@ -213,38 +252,74 @@
             out = dot(h[...], wdn[lax.rem(n, 2)]).astype(BF16)
             z[e, :, :, :, pl.ds(pl.multiple_of(i * DOWN, DOWN), DOWN)] = out.reshape(side, side, pad, DOWN)
 
-        for c in third(e):
+        @pl.when(e < final)
+        def _():
+            for c in third(e):
+                c.start()
+
+    pl.loop(0, local)(expert)
+    order = (side // 2, right, left, 0)
+    for d in order:
+        for c in third(final, d):
             c.start()
+
+    def add(e, axis, c):
+        g, back, p = ((ga, ca, pa), (gb, cb, pb))[axis]
+        weigh = jnp.where(token == g[c, pl.ds(e, 1), :], g[c, pl.ds(local + e, 1), :], 0.0).astype(BF16)
+        p[c] += dot(weigh, back[e, c].reshape(side * pad, half))
 
     pa[...] = jnp.zeros_like(pa)
     pb[...] = jnp.zeros_like(pb)
 
-    @pl.loop(0, local)
+    @pl.loop(0, final)
     def _(e):
         for c in third(e):
             c.wait()
-        for p, g, back in ((pa, ga, ca), (pb, gb, cb)):
-            for s in range(side):
-                weigh = jnp.where(token == g[s, pl.ds(e, 1), :], g[s, pl.ds(local + e, 1), :], 0.0).astype(BF16)
-                p[s] += dot(weigh, back[e, s].reshape(side * pad, half))
-
-    last = []
-    for axis, (p, t, q) in enumerate(((pa, ta, qa), (pb, tb, qb))):
-        t[...] = p[...].astype(BF16)
-        mine = (at.x, at.y)[axis]
-        for d in range(1, side):
-            c, device = at.peer(axis, d)
-            last.append(remote(t.at[c], q.at[mine], (s4s, s4r), axis * side + d, device))
-    for c in last:
+        for s in range(side):
+            add(e, 0, s)
+            add(e, 1, s)
+
+    waits = []
+
+    def send(axis, i, src, dst, d):
+        c = remote(src, dst, (s4s, s4r), axis * 6 + i, at.peer(axis, d)[1])
         c.start()
-    for c in last:
-        c.wait()
-    for axis, (p, q, lo) in enumerate(((pa, qa, 0), (pb, qb, half))):
-        mine = (at.x, at.y)[axis]
-        y = p[mine]
-        for d in range(1, side):
-            y += q[at.peer(axis, d)[0]].astype(F32)
-        y_ref[:, lo : lo + half] = (y + sh[:, lo : lo + half]).astype(BF16)
+        waits.append(c)
+        return c
+
+    through = {}
+    for d in order:
+        for c in third(final, d):
+            c.wait()
+        for axis, (p, t, q, v) in enumerate(((pa, ta, qa, va), (pb, tb, qb, vb))):
+            c = at.peer(axis, d)[0]
+            add(final, axis, c)
+            if d == side // 2:
+                t[0] = p[c].astype(BF16)
+                through[axis, right] = send(axis, 0, t.at[0, low], v.at[0], right)
+                through[axis, left] = send(axis, 1, t.at[0, high], v.at[1], left)
+            elif d == right:
+                t[1, high] = p[c, high].astype(BF16)
+                send(axis, 2, t.at[1, high], q.at[0, high], right)
+            elif d == left:
+                t[2, low] = p[c, low].astype(BF16)
+                send(axis, 3, t.at[2, low], q.at[1, low], left)
+    for axis, (p, t, q, v) in enumerate(((pa, ta, qa, va), (pb, tb, qb, vb))):
+        through[axis, right].wait_recv()
+        t[1, low] = (p[at.peer(axis, right)[0], low] + v[0].astype(F32)).astype(BF16)
+        send(axis, 4, t.at[1, low], q.at[0, low], right)
+        through[axis, left].wait_recv()
+        t[2, high] = (p[at.peer(axis, left)[0], high] + v[1].astype(F32)).astype(BF16)
+        send(axis, 5, t.at[2, high], q.at[1, high], left)
+    for axis, (p, lo) in enumerate(((pa, 0), (pb, half))):
+        cols = slice(lo, lo + half)
+        sh[:, cols] = sh[:, cols] + p[(at.x, at.y)[axis]]
+    for c in waits:
+        c.wait_send()
+        if all(c is not t for t in through.values()):
+            c.wait_recv()
+    for q, lo in ((qa, 0), (qb, half)):
+        y_ref[:, lo : lo + half] = (sh[:, lo : lo + half] + q[0].astype(F32) + q[1].astype(F32)).astype(BF16)
 
 
 def solution(mesh):
@@ -276,19 +351,23 @@
             + [pltpu.VMEM((local, side, side, pad, d_model), BF16), pltpu.VMEM((side * side * pad, ff), BF16)]
             + [staged] * 2
             + [added] * 2
-            + [gathered] * 4
+            + [pltpu.VMEM((3, tokens, half), BF16)] * 2
+            + [pltpu.VMEM((2, tokens, half), BF16)] * 2
+            + [pltpu.VMEM((2, tokens // 2, half), BF16)] * 2
             + [
                 pltpu.VMEM((tokens, d_model), F32),
                 pltpu.VMEM((DEPTH, d_model, 2 * UP), BF16),
                 pltpu.VMEM((2, ff, DOWN), BF16),
             ]
-            + [dma(4 * side)] * 2
-            + [dma(2 * local * side)] * 4
             + [dma(2 * side)] * 2
-            + [dma(local, 2)] * 2
+            + [dma(12)] * 2
+            + [dma(2 * local * side)] * 2
+            + [dma(2 * (local + side) * side)] * 2
+            + [dma(12)] * 2
+            + [dma(local, 2), dma(local + side, 2)]
             + [dma(DEPTH, 2), dma(2)],
             compiler_params=pltpu.CompilerParams(collective_id=0, has_side_effects=True, vmem_limit_bytes=67043328),
-        )(x, expert.T, slot.T, gate.T, s_gate, s_up, s_down, w_gate, w_up, w_down)
+        )(x, expert.T[:, None], slot.T[:, None], gate.T[:, None], s_gate, s_up, s_down, w_gate, w_up, w_down)
         return y[None, None]
 
     token = P("dp", "ep")

time: 159 us -> 144 us (0.906)
  Pallas kernels: 154 us -> 137 us
    pallas_call x1, Pallas kernels: 154 us -> 137 us  [body(): pl.pallas_call(functools.partial(layer_kernel, side, slots), out_shape=ja...]
    broadcast_in_dim x0 -> x3, local copies, waits for them, and re-layouts: none -> 1.8 us  [the longest x1 0.6 us: body(): gate.T[:, None]]
    unnamed x2 -> x4, local copies, waits for them, and re-layouts: 3.59 us -> 4.38 us
where the time goes in v3:
time: 144 us; the launch traced here: 143 us
  Pallas kernels  137 us (95%)
  local copies, waits for them, and re-layouts  6.18 us (4%)
    pallas_call x1, Pallas kernels, body(): pl.pallas_call(functools.partial(layer_kernel, side, slots), out_shape=ja...  137 us
    unnamed x4, local copies, waits for them, and re-layouts  4.38 us

profile of v3, /device:TPU:96, one launch (start us, length us, event | category | flops | bytes accessed | tf_op | source)
XLA Modules:
  0.0 142.9 jit_solution(15640200201297102783)
XLA Ops:
  0.0 0.7 copy.19
  0.7 0.6 broadcast_in_dim.12.ex_ref
  1.3 0.7 copy.18
  2.0 0.6 broadcast_in_dim.13.sl_ref
  2.6 0.7 copy.17
  3.3 0.6 broadcast_in_dim.14.gt_ref
  3.9 136.7 %shard_map.100 = bf16[256,2048]{1,0:T(8,128)(2,1)} custom-call(bf16[256,2048]{1,0:T(8,128)(2,1)} %bitcast.18, s32[6,1,256]{2,1,0:T(1,128)} %broadcast_in_dim.12.ex_ref, s32[6,1,256]{2,1,0:T(1,128)} %broadcast_in_dim.13.sl_ref, f32[6,1,256]{2,1,0:T(1,128)} %broadcast_in_dim.14.gt_ref, bf16[2048,2816]{1,0:T(8,128)(2,1)} %sg_ref.1, bf16[2048,2816]{1,0:T(8,128)(2,1)} %su_ref.1, ...), custom_call_target="tpu_custom_call" | custom-call | tf_op jit(solution)/shard_map/pallas_call | solution.py:343
  140.6 2.3 %copy.21 = bf16[1,1,256,2048]{3,2,1,0:T(8,128)(2,1)} copy(bf16[1,1,256,2048]{3,2,1,0:T(8,128)(2,1)} %bitcast.17) | data formatting | bytes 2097152

commit v4 on v3

--- a/solution.py
+++ b/solution.py
@@ -328,8 +328,8 @@
     dma = lambda *n: pltpu.SemaphoreType.DMA(n)
 
     def body(x, expert, slot, gate, w_gate, w_up, w_down, s_gate, s_up, s_down):
-        x, expert, slot, gate = x[0, 0], expert[0, 0], slot[0, 0], gate[0, 0]
-        tokens, top = expert.shape
+        x, tokens, top = x[0, 0], *expert.shape[2:]
+        by_choice = lambda v: v[0].transpose(2, 0, 1)
         d_model = x.shape[1]
         local, _, ff = w_gate.shape
         slots = 5 * tokens * top // (4 * local * side * side)
@@ -367,7 +367,7 @@
             + [dma(local, 2), dma(local + side, 2)]
             + [dma(DEPTH, 2), dma(2)],
             compiler_params=pltpu.CompilerParams(collective_id=0, has_side_effects=True, vmem_limit_bytes=67043328),
-        )(x, expert.T[:, None], slot.T[:, None], gate.T[:, None], s_gate, s_up, s_down, w_gate, w_up, w_down)
+        )(x, by_choice(expert), by_choice(slot), by_choice(gate), s_gate, s_up, s_down, w_gate, w_up, w_down)
         return y[None, None]
 
     token = P("dp", "ep")

time: 144 us -> 140 us (0.972)
  local copies, waits for them, and re-layouts: 6.18 us -> 2.3 us
    unnamed x4 -> x1, local copies, waits for them, and re-layouts: 4.38 us -> 2.3 us
    broadcast_in_dim x3 -> x0, local copies, waits for them, and re-layouts: 1.8 us -> none  [the longest x1 0.6 us: body(): gate.T[:, None]]
where the time goes in v4:
time: 140 us; the launch traced here: 139 us
  Pallas kernels  137 us (98%)
  local copies, waits for them, and re-layouts  2.3 us (2%)
    pallas_call x1, Pallas kernels, body(): pl.pallas_call(functools.partial(layer_kernel, side, slots), out_shape=ja...  137 us

profile of v4, /device:TPU:96, one launch (start us, length us, event | category | flops | bytes accessed | tf_op | source)
XLA Modules:
  0.0 139.0 jit_solution(12107497360543480006)
XLA Ops:
  0.0 136.7 %shard_map.100 = bf16[256,2048]{1,0:T(8,128)(2,1)} custom-call(bf16[256,2048]{1,0:T(8,128)(2,1)} %bitcast.12, s32[6,1,256]{2,1,0:T(1,128)} %bitcast.13, s32[6,1,256]{2,1,0:T(1,128)} %bitcast.14, f32[6,1,256]{2,1,0:T(1,128)} %bitcast.15, bf16[2048,2816]{1,0:T(8,128)(2,1)} %sg_ref.1, bf16[2048,2816]{1,0:T(8,128)(2,1)} %su_ref.1, bf16[2816,2048]{1,0:T(8,128)(2,1)} %sd_ref.1, ...), custom_call_target="tpu_custom_call" | custom-call | tf_op jit(solution)/shard_map/pallas_call | solution.py:343
  136.7 2.3 %copy.12 = bf16[1,1,256,2048]{3,2,1,0:T(8,128)(2,1)} copy(bf16[1,1,256,2048]{3,2,1,0:T(8,128)(2,1)} %bitcast.11) | data formatting | bytes 2097152
